TPU v7x, 32 devices: a whole 2x2x4 slice. The times are simulated.
32 devices in a mesh: chan: 8 (over z, y), beam: 4 (over x, core).
Axes of the slice: x: 2, y: 2, z: 4, core: 2. Of those that a mesh axis runs over, the one named last changes fastest.
Arguments:
- signals: bfloat16 [2048, 8192], P('chan', 'beam'), may hold values from -6 to 6
- weights: bfloat16 [3, 2, 512, 2048], P(None, None, 'beam', 'chan'), may hold values from -0.125 to 0.125
- bin_group: int32 [256], replicated, may hold values from 0 to 2
Outputs:
- formed: float32 [256, 2, 512], P('chan', None, 'beam')
All inputs are finite; a program needn't handle non-finite values.
Results may differ from a plain program's by a relative error of at most 0.0042.
Values may be sent and summed in bfloat16 or wider, within the bound.
A program may use at most 64 MiB of HBM per device.

v0:
```python
import math
import jax
import jax.numpy as jnp
from jax import lax
from jax.sharding import PartitionSpec as P


def complex_terms(weight_block, spec_block, onehot):
    selected = onehot[:, :, None, None] * spec_block[:, None, :, :]
    products = jnp.einsum(
        "gpbc,fgqc->fpqb", weight_block, selected, preferred_element_type=jnp.float32
    )
    real_part = products[:, 0, 0] - products[:, 1, 1]
    imag_part = products[:, 0, 1] + products[:, 1, 0]
    return jnp.stack([real_part, imag_part], 1)


def transform(samples, first_sample, span, total_samples, bin_count):
    block = 512
    frequency = jnp.arange(1, bin_count + 1, dtype=jnp.int32)

    def add_block(step, running):
        start = step * block
        piece = lax.dynamic_slice_in_dim(samples, start, block, 1)
        sample_index = first_sample + start + jnp.arange(block, dtype=jnp.int32)
        phases = frequency[:, None] * sample_index[None, :] % total_samples
        angles = 2.0 * math.pi / total_samples * phases.astype(jnp.float32)
        twiddle = jnp.stack([jnp.cos(angles), -jnp.sin(angles)], 1).astype(jnp.bfloat16)
        return running + lax.dot_general(
            twiddle, piece, (((2,), (1,)), ((), ())), preferred_element_type=jnp.float32
        )

    empty = jnp.zeros((bin_count, 2, samples.shape[0]), jnp.float32)
    return lax.fori_loop(0, span // block, add_block, empty)


def shards(signals, weights, bin_group):
    samples_dev = signals.shape[1]
    total_samples = samples_dev * lax.axis_size("beam")
    bin_count = bin_group.shape[0]
    set_count = weights.shape[0]
    scale = 1.0 / math.sqrt(total_samples)
    full_time = lax.all_to_all(signals, "beam", split_axis=0, concat_axis=1, tiled=True)
    partial_value = transform(full_time, 0, total_samples, total_samples, bin_count)
    own_spec = (partial_value * scale).astype(jnp.bfloat16)
    spectrum = lax.all_gather(own_spec, "beam", axis=2, tiled=True)
    bin_dev = bin_count // lax.axis_size("chan")
    set_ids = jnp.arange(set_count, dtype=jnp.int32)
    local_spec = lax.all_to_all(spectrum, "chan", split_axis=0, concat_axis=2, tiled=True)
    local_sets = lax.dynamic_slice_in_dim(bin_group, lax.axis_index("chan") * bin_dev, bin_dev)
    onehot = (local_sets[:, None] == set_ids[None, :]).astype(jnp.bfloat16)
    return complex_terms(lax.all_gather(weights, "chan", axis=3, tiled=True), local_spec, onehot)


def solution(mesh):
    in_specs = (P("chan", "beam"), P(None, None, "beam", "chan"), P())
    out_specs = P("chan", None, "beam")
    return jax.shard_map(shards, mesh=mesh, in_specs=in_specs, out_specs=out_specs, check_vma=False)
```

profile of v0, /device:TPU:0, one launch (start us, length us, event | category | flops | bytes accessed | tf_op | source)
XLA Modules:
  0.0 104.1 jit_solution(7308417566398005931)
XLA Ops:
  6.5 4.2 %all-to-all-start = ((bf16[4,64,2048]{2,1,0:T(8,128)(2,1)}), bf16[4,64,2048]{2,1,0:T(8,128)(2,1)S(1)}, u32[]{:S(2)}, u32[]{:S(2)}) async-start(bf16[4,64,2048]{2,1,0:T(8,128)(2,1)} %bitcast.45), calls=%async_computation | async-start | bytes 2097152 | tf_op jit(solution)/shard_map/all_to_all | solution.py:43
  10.8 0.0 all-gather.2.cloned.1.call-start
  10.8 1.8 %copy.38 = bf16[3,2,128,256]{3,2,0,1:T(8,128)(2,1)} copy(bf16[3,2,128,256]{3,2,1,0:T(8,128)(2,1)} %param.6) | data formatting | bytes 786432 | tf_op args[1]
  12.5 0.0 all-gather.2.cloned.1.call-update
  12.6 12.6 %all-to-all-done = bf16[4,64,2048]{2,1,0:T(8,128)(2,1)S(1)} async-done(((bf16[4,64,2048]{2,1,0:T(8,128)(2,1)}), bf16[4,64,2048]{2,1,0:T(8,128)(2,1)S(1)}, u32[]{:S(2)}, u32[]{:S(2)}) %all-to-all-start) | async-done | bytes 1048608 | tf_op jit(solution)/shard_map/all_to_all | solution.py:43
  25.2 0.1 copy.46
  25.3 0.0 copy-start
  25.3 45.1 %while.16 = (s32[]{:T(128)}, f32[256,2,64]{0,2,1:T(8,128)S(1)}, bf16[64,8192]{1,0:T(8,128)(2,1)S(1)}, s32[]{:T(128)}, s32[]{:T(128)}, /*index=5*/s32[]{:T(128)}, s32[]{:T(128)}) while((s32[]{:T(128)}, f32[256,2,64]{0,2,1:T(8,128)S(1)}, bf16[64,8192]{1,0:T(8,128)(2,1)S(1)}, s32[]{:T(128)}, s32[]{:T(128)}, /*index=5*/s32[]{:T(128)}, ...), condition=%wide.region_1.2_spmd.clone, body=%wide.region_0.1_spmd.clone.sunk | while | flops 36111112 | bytes 1382549 | solution.py:34
  25.4 2.5 %cosine_convert_fusion.2 = (bf16[256,1,512]{2,0,1:T(8,128)(2,1)S(1)}, bf16[256,1,512]{2,0,1:T(8,128)(2,1)S(1)}) fusion(s32[512]{0:T(512)S(1)} %iota_add_fusion.4, s32[256]{0:T(256)S(1)} %iota_add_fusion.5), kind=kLoop, calls=%fused_computation.14.clone.1 | loop fusion | flops 2228224 | bytes 527360 | tf_op jit(solution)/shard_map/convert
  27.8 0.3 convolution_add_fusion.2
  28.2 2.5 %cosine_convert_fusion.2 = (bf16[256,1,512]{2,0,1:T(8,128)(2,1)S(1)}, bf16[256,1,512]{2,0,1:T(8,128)(2,1)S(1)}) fusion(s32[512]{0:T(512)S(1)} %iota_add_fusion.4, s32[256]{0:T(256)S(1)} %iota_add_fusion.5), kind=kLoop, calls=%fused_computation.14.clone.1 | loop fusion | flops 2228224 | bytes 527360 | tf_op jit(solution)/shard_map/convert
  30.7 0.3 convolution_add_fusion.2
  31.0 2.5 %cosine_convert_fusion.2 = (bf16[256,1,512]{2,0,1:T(8,128)(2,1)S(1)}, bf16[256,1,512]{2,0,1:T(8,128)(2,1)S(1)}) fusion(s32[512]{0:T(512)S(1)} %iota_add_fusion.4, s32[256]{0:T(256)S(1)} %iota_add_fusion.5), kind=kLoop, calls=%fused_computation.14.clone.1 | loop fusion | flops 2228224 | bytes 527360 | tf_op jit(solution)/shard_map/convert
  33.5 0.3 convolution_add_fusion.2
  33.8 2.5 %cosine_convert_fusion.2 = (bf16[256,1,512]{2,0,1:T(8,128)(2,1)S(1)}, bf16[256,1,512]{2,0,1:T(8,128)(2,1)S(1)}) fusion(s32[512]{0:T(512)S(1)} %iota_add_fusion.4, s32[256]{0:T(256)S(1)} %iota_add_fusion.5), kind=kLoop, calls=%fused_computation.14.clone.1 | loop fusion | flops 2228224 | bytes 527360 | tf_op jit(solution)/shard_map/convert
  36.3 0.3 convolution_add_fusion.2
  36.6 2.5 %cosine_convert_fusion.2 = (bf16[256,1,512]{2,0,1:T(8,128)(2,1)S(1)}, bf16[256,1,512]{2,0,1:T(8,128)(2,1)S(1)}) fusion(s32[512]{0:T(512)S(1)} %iota_add_fusion.4, s32[256]{0:T(256)S(1)} %iota_add_fusion.5), kind=kLoop, calls=%fused_computation.14.clone.1 | loop fusion | flops 2228224 | bytes 527360 | tf_op jit(solution)/shard_map/convert
  39.1 0.3 convolution_add_fusion.2
  39.5 2.5 %cosine_convert_fusion.2 = (bf16[256,1,512]{2,0,1:T(8,128)(2,1)S(1)}, bf16[256,1,512]{2,0,1:T(8,128)(2,1)S(1)}) fusion(s32[512]{0:T(512)S(1)} %iota_add_fusion.4, s32[256]{0:T(256)S(1)} %iota_add_fusion.5), kind=kLoop, calls=%fused_computation.14.clone.1 | loop fusion | flops 2228224 | bytes 527360 | tf_op jit(solution)/shard_map/convert
  41.9 0.3 convolution_add_fusion.2
  42.3 2.5 %cosine_convert_fusion.2 = (bf16[256,1,512]{2,0,1:T(8,128)(2,1)S(1)}, bf16[256,1,512]{2,0,1:T(8,128)(2,1)S(1)}) fusion(s32[512]{0:T(512)S(1)} %iota_add_fusion.4, s32[256]{0:T(256)S(1)} %iota_add_fusion.5), kind=kLoop, calls=%fused_computation.14.clone.1 | loop fusion | flops 2228224 | bytes 527360 | tf_op jit(solution)/shard_map/convert
  44.8 0.3 convolution_add_fusion.2
  45.1 2.5 %cosine_convert_fusion.2 = (bf16[256,1,512]{2,0,1:T(8,128)(2,1)S(1)}, bf16[256,1,512]{2,0,1:T(8,128)(2,1)S(1)}) fusion(s32[512]{0:T(512)S(1)} %iota_add_fusion.4, s32[256]{0:T(256)S(1)} %iota_add_fusion.5), kind=kLoop, calls=%fused_computation.14.clone.1 | loop fusion | flops 2228224 | bytes 527360 | tf_op jit(solution)/shard_map/convert
  47.6 0.3 convolution_add_fusion.2
  47.9 2.5 %cosine_convert_fusion.2 = (bf16[256,1,512]{2,0,1:T(8,128)(2,1)S(1)}, bf16[256,1,512]{2,0,1:T(8,128)(2,1)S(1)}) fusion(s32[512]{0:T(512)S(1)} %iota_add_fusion.4, s32[256]{0:T(256)S(1)} %iota_add_fusion.5), kind=kLoop, calls=%fused_computation.14.clone.1 | loop fusion | flops 2228224 | bytes 527360 | tf_op jit(solution)/shard_map/convert
  50.4 0.3 convolution_add_fusion.2
  50.8 2.5 %cosine_convert_fusion.2 = (bf16[256,1,512]{2,0,1:T(8,128)(2,1)S(1)}, bf16[256,1,512]{2,0,1:T(8,128)(2,1)S(1)}) fusion(s32[512]{0:T(512)S(1)} %iota_add_fusion.4, s32[256]{0:T(256)S(1)} %iota_add_fusion.5), kind=kLoop, calls=%fused_computation.14.clone.1 | loop fusion | flops 2228224 | bytes 527360 | tf_op jit(solution)/shard_map/convert
  53.2 0.3 convolution_add_fusion.2
  53.6 2.5 %cosine_convert_fusion.2 = (bf16[256,1,512]{2,0,1:T(8,128)(2,1)S(1)}, bf16[256,1,512]{2,0,1:T(8,128)(2,1)S(1)}) fusion(s32[512]{0:T(512)S(1)} %iota_add_fusion.4, s32[256]{0:T(256)S(1)} %iota_add_fusion.5), kind=kLoop, calls=%fused_computation.14.clone.1 | loop fusion | flops 2228224 | bytes 527360 | tf_op jit(solution)/shard_map/convert
  56.0 0.3 convolution_add_fusion.2
  56.4 2.5 %cosine_convert_fusion.2 = (bf16[256,1,512]{2,0,1:T(8,128)(2,1)S(1)}, bf16[256,1,512]{2,0,1:T(8,128)(2,1)S(1)}) fusion(s32[512]{0:T(512)S(1)} %iota_add_fusion.4, s32[256]{0:T(256)S(1)} %iota_add_fusion.5), kind=kLoop, calls=%fused_computation.14.clone.1 | loop fusion | flops 2228224 | bytes 527360 | tf_op jit(solution)/shard_map/convert
  58.9 0.3 convolution_add_fusion.2
  59.2 2.5 %cosine_convert_fusion.2 = (bf16[256,1,512]{2,0,1:T(8,128)(2,1)S(1)}, bf16[256,1,512]{2,0,1:T(8,128)(2,1)S(1)}) fusion(s32[512]{0:T(512)S(1)} %iota_add_fusion.4, s32[256]{0:T(256)S(1)} %iota_add_fusion.5), kind=kLoop, calls=%fused_computation.14.clone.1 | loop fusion | flops 2228224 | bytes 527360 | tf_op jit(solution)/shard_map/convert
  61.7 0.3 convolution_add_fusion.2
  62.0 2.5 %cosine_convert_fusion.2 = (bf16[256,1,512]{2,0,1:T(8,128)(2,1)S(1)}, bf16[256,1,512]{2,0,1:T(8,128)(2,1)S(1)}) fusion(s32[512]{0:T(512)S(1)} %iota_add_fusion.4, s32[256]{0:T(256)S(1)} %iota_add_fusion.5), kind=kLoop, calls=%fused_computation.14.clone.1 | loop fusion | flops 2228224 | bytes 527360 | tf_op jit(solution)/shard_map/convert
  64.5 0.3 convolution_add_fusion.2
  64.9 2.5 %cosine_convert_fusion.2 = (bf16[256,1,512]{2,0,1:T(8,128)(2,1)S(1)}, bf16[256,1,512]{2,0,1:T(8,128)(2,1)S(1)}) fusion(s32[512]{0:T(512)S(1)} %iota_add_fusion.4, s32[256]{0:T(256)S(1)} %iota_add_fusion.5), kind=kLoop, calls=%fused_computation.14.clone.1 | loop fusion | flops 2228224 | bytes 527360 | tf_op jit(solution)/shard_map/convert
  67.3 0.3 convolution_add_fusion.2
  67.7 2.5 %cosine_convert_fusion.2 = (bf16[256,1,512]{2,0,1:T(8,128)(2,1)S(1)}, bf16[256,1,512]{2,0,1:T(8,128)(2,1)S(1)}) fusion(s32[512]{0:T(512)S(1)} %iota_add_fusion.4, s32[256]{0:T(256)S(1)} %iota_add_fusion.5), kind=kLoop, calls=%fused_computation.14.clone.1 | loop fusion | flops 2228224 | bytes 527360 | tf_op jit(solution)/shard_map/convert
  70.1 0.3 convolution_add_fusion.2
  70.5 0.1 copy.34
  70.6 5.8 %all_gather.6 = bf16[256,2,256]{0,1,2:T(2,128)(2,1)S(1)} all-gather(bf16[256,2,64]{0,1,2:T(2,128)(2,1)S(1)} %copy.34), channel_id=1, replica_groups=mesh['chan'=8,'beam'=4] {'beam'}, dimensions={2}, use_global_device_ids=true | all-gather | bytes 327680 | tf_op jit(solution)/shard_map/all_gather | solution.py:46
  76.3 1.1 %copy.35 = bf16[256,2,256]{2,1,0:T(2,128)(2,1)} copy(bf16[256,2,256]{0,1,2:T(2,128)(2,1)S(1)} %all_gather.6) | data formatting | bytes 524288 | tf_op jit(solution)/shard_map/all_gather | solution.py:46
  77.5 6.6 %all-to-all-start.1 = ((bf16[256,2,256]{2,1,0:T(2,128)(2,1)}), bf16[256,2,256]{2,1,0:T(2,128)(2,1)S(1)}, u32[]{:S(2)}, u32[]{:S(2)}) async-start(bf16[256,2,256]{2,1,0:T(2,128)(2,1)} %copy.35), calls=%async_computation.1 | async-start | bytes 524288 | tf_op jit(solution)/shard_map/all_to_all | solution.py:49
  84.0 0.0 copy-done
  84.0 0.1 dynamic_slice.13
  84.1 9.3 %all-to-all-done.1 = bf16[256,2,256]{2,1,0:T(2,128)(2,1)S(1)} async-done(((bf16[256,2,256]{2,1,0:T(2,128)(2,1)}), bf16[256,2,256]{2,1,0:T(2,128)(2,1)S(1)}, u32[]{:S(2)}, u32[]{:S(2)}) %all-to-all-start.1) | async-done | bytes 262176 | tf_op jit(solution)/shard_map/all_to_all | solution.py:49
  93.5 0.0 all-gather.2.cloned.1.call-done
  93.6 3.0 %fusion.14 = f32[32,2,2,128]{3,0,1,2:T(8,128)S(1)} fusion(bf16[3,2,128,2048]{3,2,0,1:T(8,128)(2,1)} %all-gather.2.cloned.1.call-done, bf16[32,2,2048]{2,0,1:T(8,128)(2,1)S(1)} %bitcast.44, bf16[32,3]{0,1:T(4,128)(2,1)S(1)} %fusion.24), kind=kOutput, calls=%fused_computation.23 | convolution fusion | flops 202899456 | bytes 3473600 | tf_op jit(solution)/shard_map/gpbc,fgqc->fpqb/dot_general | solution.py:10
  96.6 0.6 copy.41
  (40 shorter events, 0.2 us)
Async XLA Ops:
  6.5 18.7 %all-to-all-start = ((bf16[4,64,2048]{2,1,0:T(8,128)(2,1)}), bf16[4,64,2048]{2,1,0:T(8,128)(2,1)S(1)}, u32[]{:S(2)}, u32[]{:S(2)}) async-start(bf16[4,64,2048]{2,1,0:T(8,128)(2,1)} %bitcast.45), calls=%async_computation | async-start | bytes 2097152 | tf_op jit(solution)/shard_map/all_to_all | solution.py:43
  10.8 82.8 %all-gather.2.cloned.1.call-start = ((), (), s32[]{:S(2)}) async-start(), calls=%async_computation.2 | async-start | bytes 3538944 | tf_op jit(solution)/shard_map/all_gather | solution.py:52
  25.3 58.7 %copy-start = (s32[256]{0:T(256)S(1)}, s32[256]{0:T(256)}, u32[]{:S(2)}) copy-start(s32[256]{0:T(256)} %param.7) | copy-start | bytes 3076
  77.5 16.0 %all-to-all-start.1 = ((bf16[256,2,256]{2,1,0:T(2,128)(2,1)}), bf16[256,2,256]{2,1,0:T(2,128)(2,1)S(1)}, u32[]{:S(2)}, u32[]{:S(2)}) async-start(bf16[256,2,256]{2,1,0:T(2,128)(2,1)} %copy.35), calls=%async_computation.1 | async-start | bytes 524288 | tf_op jit(solution)/shard_map/all_to_all | solution.py:49
Sparse Core Ops, SparseCore 0:
  13.6 65.2 all-gather.1
where the time goes:
time: 104 us
  other arithmetic  39.5 us (38%)
  waiting for transfers between devices  22 us (21%)
  between operations  13.5 us (13%)
  starting transfers between devices  10.8 us (10%)
  matrix products  7.83 us (8%)
  blocking collectives  5.78 us (6%)
  local copies, waits for them, and re-layouts  3.82 us (4%)
    another operation x16, other arithmetic  39.3 us
    all_to_all x1, waiting for transfers between devices, shards(): lax.all_to_all(signals, 'beam', split_axis=0, concat_axis=1, tiled=True)  12.6 us
    all_to_all x1, waiting for transfers between devices, shards(): lax.all_to_all(spectrum, 'chan', split_axis=0, concat_axis=2, tiled=True)  9.34 us
    all_to_all x1, starting transfers between devices, shards(): lax.all_to_all(spectrum, 'chan', split_axis=0, concat_axis=2, tiled=True)  6.57 us
    all_gather x1, blocking collectives, shards(): spectrum = lax.all_gather(own_spec, 'beam', axis=2, tiled=True)  5.78 us
    dot_general x16, matrix products, add_block(): lax.dot_general(twiddle, piece, (((2,), (1,)), ((), ())), preferred_eleme...  4.86 us
    all_to_all x1, starting transfers between devices, shards(): lax.all_to_all(signals, 'beam', split_axis=0, concat_axis=1, tiled=True)  4.24 us
    dot_general x1, matrix products, complex_terms(): jnp.einsum('gpbc,fgqc->fpqb', weight_block, selected, preferred_element_t...  2.97 us
  transfers between devices with their start and end apart: 3, of which 2 were waited for; matrix products, arithmetic and copies ran while one was open for 46% of the time, Pallas kernels for 0%

commit v1 on v0

--- a/solution.py
+++ b/solution.py
@@ -46,7 +46,10 @@
     spectrum = lax.all_gather(own_spec, "beam", axis=2, tiled=True)
     bin_dev = bin_count // lax.axis_size("chan")
     set_ids = jnp.arange(set_count, dtype=jnp.int32)
-    local_spec = lax.all_to_all(spectrum, "chan", split_axis=0, concat_axis=2, tiled=True)
+    local_spec = jnp.concatenate(
+        lax.all_to_all(jnp.stack(jnp.split(spectrum, lax.axis_size("chan"), axis=0)), "chan", 0, 0),
+        axis=2,
+    )
     local_sets = lax.dynamic_slice_in_dim(bin_group, lax.axis_index("chan") * bin_dev, bin_dev)
     onehot = (local_sets[:, None] == set_ids[None, :]).astype(jnp.bfloat16)
     return complex_terms(lax.all_gather(weights, "chan", axis=3, tiled=True), local_spec, onehot)

time: 104 us -> 110 us (1.058)
  local copies, waits for them, and re-layouts: 3.82 us -> 9.29 us
    unnamed x3 -> x10, local copies, waits for them, and re-layouts: 1.77 us -> 6.08 us
    another operation x0 -> x10, local copies, waits for them, and re-layouts: none -> 2.3 us  [shards(): jnp.stack(jnp.split(spectrum, lax.axis_size('chan'), axis=0))]
    all_gather x1 -> x0, local copies, waits for them, and re-layouts: 1.12 us -> none  [shards(): spectrum = lax.all_gather(own_spec, 'beam', axis=2, tiled=True)]
  transfers between devices with their start and end apart: 3 -> 3, of which waited for: 2 -> 2; matrix products, arithmetic and copies ran while one was open for 46% -> 48% of each run, Pallas kernels for 0% -> 0%
where the time goes in v1:
time: 110 us
  other arithmetic  39.5 us (36%)
  waiting for transfers between devices  22 us (20%)
  between operations  13.5 us (12%)
  starting transfers between devices  10.8 us (10%)
  local copies, waits for them, and re-layouts  9.29 us (8%)
  matrix products  7.86 us (7%)
  blocking collectives  5.78 us (5%)
    another operation x16, other arithmetic  39.3 us
    all_to_all x1, waiting for transfers between devices, shards(): lax.all_to_all(signals, 'beam', split_axis=0, concat_axis=1, tiled=True)  12.6 us
    all_to_all x1, waiting for transfers between devices, shards(): lax.all_to_all(jnp.stack(jnp.split(spectrum, lax.axis_size('chan'), axis=...  9.34 us
    all_to_all x1, starting transfers between devices, shards(): lax.all_to_all(jnp.stack(jnp.split(spectrum, lax.axis_size('chan'), axis=...  6.56 us
    unnamed x10, local copies, waits for them, and re-layouts  6.08 us
    all_gather x1, blocking collectives, shards(): spectrum = lax.all_gather(own_spec, 'beam', axis=2, tiled=True)  5.78 us
    dot_general x16, matrix products, add_block(): lax.dot_general(twiddle, piece, (((2,), (1,)), ((), ())), preferred_eleme...  4.88 us
    all_to_all x1, starting transfers between devices, shards(): lax.all_to_all(signals, 'beam', split_axis=0, concat_axis=1, tiled=True)  4.24 us
  transfers between devices with their start and end apart: 3, of which 2 were waited for; matrix products, arithmetic and copies ran while one was open for 48% of the time, Pallas kernels for 0%

profile of v1, /device:TPU:0, one launch (start us, length us, event | category | flops | bytes accessed | tf_op | source)
XLA Modules:
  0.0 109.6 jit_solution(3557003366026695402)
XLA Ops:
  6.5 4.2 %all-to-all-start = ((bf16[4,64,2048]{2,1,0:T(8,128)(2,1)}), bf16[4,64,2048]{2,1,0:T(8,128)(2,1)S(1)}, u32[]{:S(2)}, u32[]{:S(2)}) async-start(bf16[4,64,2048]{2,1,0:T(8,128)(2,1)} %bitcast.59), calls=%async_computation | async-start | bytes 2097152 | tf_op jit(solution)/shard_map/all_to_all | solution.py:43
  10.8 1.8 %copy.54 = bf16[3,2,128,256]{3,2,0,1:T(8,128)(2,1)} copy(bf16[3,2,128,256]{3,2,1,0:T(8,128)(2,1)} %param.6) | data formatting | bytes 786432 | tf_op args[1]
  12.5 0.0 all-gather.2.cloned.1.call-update
  12.6 12.6 %all-to-all-done = bf16[4,64,2048]{2,1,0:T(8,128)(2,1)S(1)} async-done(((bf16[4,64,2048]{2,1,0:T(8,128)(2,1)}), bf16[4,64,2048]{2,1,0:T(8,128)(2,1)S(1)}, u32[]{:S(2)}, u32[]{:S(2)}) %all-to-all-start) | async-done | bytes 1048608 | tf_op jit(solution)/shard_map/all_to_all | solution.py:43
  25.2 0.1 copy.62
  25.3 45.2 %while.16 = (s32[]{:T(128)}, f32[256,2,64]{0,2,1:T(8,128)S(1)}, bf16[64,8192]{1,0:T(8,128)(2,1)S(1)}, s32[]{:T(128)}, s32[]{:T(128)}, /*index=5*/s32[]{:T(128)}, s32[]{:T(128)}) while((s32[]{:T(128)}, f32[256,2,64]{0,2,1:T(8,128)S(1)}, bf16[64,8192]{1,0:T(8,128)(2,1)S(1)}, s32[]{:T(128)}, s32[]{:T(128)}, /*index=5*/s32[]{:T(128)}, ...), condition=%wide.region_1.2_spmd.clone, body=%wide.region_0.1_spmd.clone.sunk | while | flops 36111112 | bytes 1382541 | solution.py:34
  25.4 2.5 %cosine_convert_fusion.2 = (bf16[256,1,512]{2,0,1:T(8,128)(2,1)S(1)}, bf16[256,1,512]{2,0,1:T(8,128)(2,1)S(1)}) fusion(s32[512]{0:T(512)S(1)} %iota_add_fusion.4, s32[256]{0:T(256)S(1)} %iota_add_fusion.5), kind=kLoop, calls=%fused_computation.14.clone.1 | loop fusion | flops 2228224 | bytes 527360 | tf_op jit(solution)/shard_map/convert
  27.8 0.3 convolution_add_fusion.2
  28.2 2.5 %cosine_convert_fusion.2 = (bf16[256,1,512]{2,0,1:T(8,128)(2,1)S(1)}, bf16[256,1,512]{2,0,1:T(8,128)(2,1)S(1)}) fusion(s32[512]{0:T(512)S(1)} %iota_add_fusion.4, s32[256]{0:T(256)S(1)} %iota_add_fusion.5), kind=kLoop, calls=%fused_computation.14.clone.1 | loop fusion | flops 2228224 | bytes 527360 | tf_op jit(solution)/shard_map/convert
  30.6 0.3 convolution_add_fusion.2
  31.0 2.5 %cosine_convert_fusion.2 = (bf16[256,1,512]{2,0,1:T(8,128)(2,1)S(1)}, bf16[256,1,512]{2,0,1:T(8,128)(2,1)S(1)}) fusion(s32[512]{0:T(512)S(1)} %iota_add_fusion.4, s32[256]{0:T(256)S(1)} %iota_add_fusion.5), kind=kLoop, calls=%fused_computation.14.clone.1 | loop fusion | flops 2228224 | bytes 527360 | tf_op jit(solution)/shard_map/convert
  33.5 0.3 convolution_add_fusion.2
  33.8 2.5 %cosine_convert_fusion.2 = (bf16[256,1,512]{2,0,1:T(8,128)(2,1)S(1)}, bf16[256,1,512]{2,0,1:T(8,128)(2,1)S(1)}) fusion(s32[512]{0:T(512)S(1)} %iota_add_fusion.4, s32[256]{0:T(256)S(1)} %iota_add_fusion.5), kind=kLoop, calls=%fused_computation.14.clone.1 | loop fusion | flops 2228224 | bytes 527360 | tf_op jit(solution)/shard_map/convert
  36.3 0.3 convolution_add_fusion.2
  36.7 2.5 %cosine_convert_fusion.2 = (bf16[256,1,512]{2,0,1:T(8,128)(2,1)S(1)}, bf16[256,1,512]{2,0,1:T(8,128)(2,1)S(1)}) fusion(s32[512]{0:T(512)S(1)} %iota_add_fusion.4, s32[256]{0:T(256)S(1)} %iota_add_fusion.5), kind=kLoop, calls=%fused_computation.14.clone.1 | loop fusion | flops 2228224 | bytes 527360 | tf_op jit(solution)/shard_map/convert
  39.1 0.3 convolution_add_fusion.2
  39.5 2.5 %cosine_convert_fusion.2 = (bf16[256,1,512]{2,0,1:T(8,128)(2,1)S(1)}, bf16[256,1,512]{2,0,1:T(8,128)(2,1)S(1)}) fusion(s32[512]{0:T(512)S(1)} %iota_add_fusion.4, s32[256]{0:T(256)S(1)} %iota_add_fusion.5), kind=kLoop, calls=%fused_computation.14.clone.1 | loop fusion | flops 2228224 | bytes 527360 | tf_op jit(solution)/shard_map/convert
  41.9 0.3 convolution_add_fusion.2
  42.3 2.5 %cosine_convert_fusion.2 = (bf16[256,1,512]{2,0,1:T(8,128)(2,1)S(1)}, bf16[256,1,512]{2,0,1:T(8,128)(2,1)S(1)}) fusion(s32[512]{0:T(512)S(1)} %iota_add_fusion.4, s32[256]{0:T(256)S(1)} %iota_add_fusion.5), kind=kLoop, calls=%fused_computation.14.clone.1 | loop fusion | flops 2228224 | bytes 527360 | tf_op jit(solution)/shard_map/convert
  44.8 0.3 convolution_add_fusion.2
  45.1 2.5 %cosine_convert_fusion.2 = (bf16[256,1,512]{2,0,1:T(8,128)(2,1)S(1)}, bf16[256,1,512]{2,0,1:T(8,128)(2,1)S(1)}) fusion(s32[512]{0:T(512)S(1)} %iota_add_fusion.4, s32[256]{0:T(256)S(1)} %iota_add_fusion.5), kind=kLoop, calls=%fused_computation.14.clone.1 | loop fusion | flops 2228224 | bytes 527360 | tf_op jit(solution)/shard_map/convert
  47.6 0.3 convolution_add_fusion.2
  48.0 2.5 %cosine_convert_fusion.2 = (bf16[256,1,512]{2,0,1:T(8,128)(2,1)S(1)}, bf16[256,1,512]{2,0,1:T(8,128)(2,1)S(1)}) fusion(s32[512]{0:T(512)S(1)} %iota_add_fusion.4, s32[256]{0:T(256)S(1)} %iota_add_fusion.5), kind=kLoop, calls=%fused_computation.14.clone.1 | loop fusion | flops 2228224 | bytes 527360 | tf_op jit(solution)/shard_map/convert
  50.4 0.3 convolution_add_fusion.2
  50.8 2.5 %cosine_convert_fusion.2 = (bf16[256,1,512]{2,0,1:T(8,128)(2,1)S(1)}, bf16[256,1,512]{2,0,1:T(8,128)(2,1)S(1)}) fusion(s32[512]{0:T(512)S(1)} %iota_add_fusion.4, s32[256]{0:T(256)S(1)} %iota_add_fusion.5), kind=kLoop, calls=%fused_computation.14.clone.1 | loop fusion | flops 2228224 | bytes 527360 | tf_op jit(solution)/shard_map/convert
  53.2 0.3 convolution_add_fusion.2
  53.6 2.5 %cosine_convert_fusion.2 = (bf16[256,1,512]{2,0,1:T(8,128)(2,1)S(1)}, bf16[256,1,512]{2,0,1:T(8,128)(2,1)S(1)}) fusion(s32[512]{0:T(512)S(1)} %iota_add_fusion.4, s32[256]{0:T(256)S(1)} %iota_add_fusion.5), kind=kLoop, calls=%fused_computation.14.clone.1 | loop fusion | flops 2228224 | bytes 527360 | tf_op jit(solution)/shard_map/convert
  56.1 0.3 convolution_add_fusion.2
  56.4 2.5 %cosine_convert_fusion.2 = (bf16[256,1,512]{2,0,1:T(8,128)(2,1)S(1)}, bf16[256,1,512]{2,0,1:T(8,128)(2,1)S(1)}) fusion(s32[512]{0:T(512)S(1)} %iota_add_fusion.4, s32[256]{0:T(256)S(1)} %iota_add_fusion.5), kind=kLoop, calls=%fused_computation.14.clone.1 | loop fusion | flops 2228224 | bytes 527360 | tf_op jit(solution)/shard_map/convert
  58.9 0.3 convolution_add_fusion.2
  59.3 2.5 %cosine_convert_fusion.2 = (bf16[256,1,512]{2,0,1:T(8,128)(2,1)S(1)}, bf16[256,1,512]{2,0,1:T(8,128)(2,1)S(1)}) fusion(s32[512]{0:T(512)S(1)} %iota_add_fusion.4, s32[256]{0:T(256)S(1)} %iota_add_fusion.5), kind=kLoop, calls=%fused_computation.14.clone.1 | loop fusion | flops 2228224 | bytes 527360 | tf_op jit(solution)/shard_map/convert
  61.7 0.3 convolution_add_fusion.2
  62.1 2.5 %cosine_convert_fusion.2 = (bf16[256,1,512]{2,0,1:T(8,128)(2,1)S(1)}, bf16[256,1,512]{2,0,1:T(8,128)(2,1)S(1)}) fusion(s32[512]{0:T(512)S(1)} %iota_add_fusion.4, s32[256]{0:T(256)S(1)} %iota_add_fusion.5), kind=kLoop, calls=%fused_computation.14.clone.1 | loop fusion | flops 2228224 | bytes 527360 | tf_op jit(solution)/shard_map/convert
  64.5 0.3 convolution_add_fusion.2
  64.9 2.5 %cosine_convert_fusion.2 = (bf16[256,1,512]{2,0,1:T(8,128)(2,1)S(1)}, bf16[256,1,512]{2,0,1:T(8,128)(2,1)S(1)}) fusion(s32[512]{0:T(512)S(1)} %iota_add_fusion.4, s32[256]{0:T(256)S(1)} %iota_add_fusion.5), kind=kLoop, calls=%fused_computation.14.clone.1 | loop fusion | flops 2228224 | bytes 527360 | tf_op jit(solution)/shard_map/convert
  67.4 0.3 convolution_add_fusion.2
  67.7 2.5 %cosine_convert_fusion.2 = (bf16[256,1,512]{2,0,1:T(8,128)(2,1)S(1)}, bf16[256,1,512]{2,0,1:T(8,128)(2,1)S(1)}) fusion(s32[512]{0:T(512)S(1)} %iota_add_fusion.4, s32[256]{0:T(256)S(1)} %iota_add_fusion.5), kind=kLoop, calls=%fused_computation.14.clone.1 | loop fusion | flops 2228224 | bytes 527360 | tf_op jit(solution)/shard_map/convert
  70.2 0.3 convolution_add_fusion.2
  70.5 0.0 copy-start
  70.6 0.1 copy.44
  70.6 5.8 %all_gather.6 = bf16[256,2,256]{0,1,2:T(2,128)(2,1)S(1)} all-gather(bf16[256,2,64]{0,1,2:T(2,128)(2,1)S(1)} %copy.44), channel_id=1, replica_groups=mesh['chan'=8,'beam'=4] {'beam'}, dimensions={2}, use_global_device_ids=true | all-gather | bytes 327680 | tf_op jit(solution)/shard_map/all_gather | solution.py:46
  76.4 1.0 slice_bitcast_fusion
  77.4 0.1 copy.45
  77.5 0.1 copy.46
  77.6 0.1 copy.47
  77.7 0.1 copy.48
  77.8 0.1 copy.49
  77.9 0.1 copy.50
  77.9 0.1 copy.51
  78.0 0.1 copy.52
  78.1 0.6 constant_dynamic-update-slice_fusion.7
  78.8 0.6 constant_dynamic-update-slice_fusion.6
  79.4 0.6 constant_dynamic-update-slice_fusion.5
  80.0 0.6 constant_dynamic-update-slice_fusion.4
  80.6 0.6 constant_dynamic-update-slice_fusion.3
  81.2 0.6 constant_dynamic-update-slice_fusion.2
  81.8 0.6 constant_dynamic-update-slice_fusion.1
  82.4 0.6 constant_dynamic-update-slice_fusion
  83.0 6.6 %all-to-all-start.1 = ((bf16[8,32,2,256]{3,1,2,0:T(8,128)(2,1)}), bf16[8,32,2,256]{3,1,2,0:T(8,128)(2,1)S(1)}, u32[]{:S(2)}, u32[]{:S(2)}) async-start(bf16[8,32,2,256]{3,1,2,0:T(8,128)(2,1)} %constant_dynamic-update-slice_fusion), calls=%async_computation.1 | async-start | bytes 524288 | tf_op jit(solution)/shard_map/all_to_all | solution.py:50
  89.6 0.1 dynamic_slice.13
  89.7 9.3 %all-to-all-done.1 = bf16[8,32,2,256]{3,1,2,0:T(8,128)(2,1)S(1)} async-done(((bf16[8,32,2,256]{3,1,2,0:T(8,128)(2,1)}), bf16[8,32,2,256]{3,1,2,0:T(8,128)(2,1)S(1)}, u32[]{:S(2)}, u32[]{:S(2)}) %all-to-all-start.1) | async-done | bytes 262176 | tf_op jit(solution)/shard_map/all_to_all | solution.py:50
  99.0 0.0 all-gather.2.cloned.1.call-done
  99.1 3.0 %fusion.14 = f32[32,2,2,128]{3,0,1,2:T(8,128)S(1)} fusion(bf16[3,2,128,2048]{3,2,0,1:T(8,128)(2,1)} %all-gather.2.cloned.1.call-done, bf16[32,2,2048]{2,0,1:T(8,128)(2,1)S(1)} %bitcast.58, bf16[32,3]{0,1:T(4,128)(2,1)S(1)} %fusion.24), kind=kOutput, calls=%fused_computation.23 | convolution fusion | flops 202899456 | bytes 3473600 | tf_op jit(solution)/shard_map/gpbc,fgqc->fpqb/dot_general | solution.py:10
  102.1 0.6 copy.57
  (41 shorter events, 0.2 us)
Async XLA Ops:
  6.5 18.7 %all-to-all-start = ((bf16[4,64,2048]{2,1,0:T(8,128)(2,1)}), bf16[4,64,2048]{2,1,0:T(8,128)(2,1)S(1)}, u32[]{:S(2)}, u32[]{:S(2)}) async-start(bf16[4,64,2048]{2,1,0:T(8,128)(2,1)} %bitcast.59), calls=%async_computation | async-start | bytes 2097152 | tf_op jit(solution)/shard_map/all_to_all | solution.py:43
  10.8 88.3 %all-gather.2.cloned.1.call-start = ((), (), s32[]{:S(2)}) async-start(), calls=%async_computation.2 | async-start | bytes 3538944 | tf_op jit(solution)/shard_map/all_gather | solution.py:55
  70.5 19.1 %copy-start = (s32[256]{0:T(256)S(1)}, s32[256]{0:T(256)}, u32[]{:S(2)}) copy-start(s32[256]{0:T(256)} %param.7) | copy-start | bytes 3076
  83.0 16.0 %all-to-all-start.1 = ((bf16[8,32,2,256]{3,1,2,0:T(8,128)(2,1)}), bf16[8,32,2,256]{3,1,2,0:T(8,128)(2,1)S(1)}, u32[]{:S(2)}, u32[]{:S(2)}) async-start(bf16[8,32,2,256]{3,1,2,0:T(8,128)(2,1)} %constant_dynamic-update-slice_fusion), calls=%async_computation.1 | async-start | bytes 524288 | tf_op jit(solution)/shard_map/all_to_all | solution.py:50
Sparse Core Ops, SparseCore 0:
  13.6 65.2 all-gather.1
